TPU v7x, 32 devices: a whole 2x2x4 slice. The times are simulated.
32 devices in a mesh: fsdp: 16 (over z, y, core), dp: 2 (over x).
Axes of the slice: x: 2, y: 2, z: 4, core: 2. Of those that a mesh axis runs over, the one named last changes fastest.
Arguments:
- block_input: bfloat16 [160, 416, 768], P(('fsdp', 'dp')), may hold values from -6 to 6
- segment_ids: int32 [160, 416], P(('fsdp', 'dp')), may hold values from -1 to 24, as said below
- ln1_gain: bfloat16 [768], P('fsdp'), may hold values from 0.099609375 to 1.8984375
- ln1_bias: bfloat16 [768], P('fsdp'), may hold values from -3 to 3
- qkv_weight: bfloat16 [768, 2304], P('fsdp'), may hold values from -0.21875 to 0.21875
- qv_bias: bfloat16 [1536], P('fsdp'), may hold values from -3 to 3
- out_weight: bfloat16 [768, 768], P('fsdp'), may hold values from -0.875 to 0.875
- out_bias: bfloat16 [768], P('fsdp'), may hold values from -3 to 3
- ln2_gain: bfloat16 [768], P('fsdp'), may hold values from 0.099609375 to 1.8984375
- ln2_bias: bfloat16 [768], P('fsdp'), may hold values from -3 to 3
- up_weight: bfloat16 [768, 3072], P('fsdp'), may hold values from -0.21875 to 0.21875
- up_bias: bfloat16 [3072], P('fsdp'), may hold values from -3 to 3
- down_weight: bfloat16 [3072, 768], P('fsdp'), may hold values from -0.109375 to 0.109375
- down_bias: bfloat16 [768], P('fsdp'), may hold values from -3 to 3
- out_cotangent: bfloat16 [160, 416, 768], P(('fsdp', 'dp')), may hold values from -6 to 6
Outputs:
- block_output: bfloat16 [160, 416, 768], P(('fsdp', 'dp'))
- input_grad: bfloat16 [160, 416, 768], P(('fsdp', 'dp'))
- ln1_gain_grad: float32 [768], P('fsdp')
- ln1_bias_grad: float32 [768], P('fsdp')
- qkv_weight_grad: float32 [768, 2304], P('fsdp')
- qv_bias_grad: float32 [1536], P('fsdp')
- out_weight_grad: float32 [768, 768], P('fsdp')
- out_bias_grad: float32 [768], P('fsdp')
- ln2_gain_grad: float32 [768], P('fsdp')
- ln2_bias_grad: float32 [768], P('fsdp')
- up_weight_grad: float32 [768, 3072], P('fsdp')
- up_bias_grad: float32 [3072], P('fsdp')
- down_weight_grad: float32 [3072, 768], P('fsdp')
- down_bias_grad: float32 [768], P('fsdp')
Inputs may be any that keep to these rules, and one draw needn't show every extreme that they name: `segment_ids`: each packed row holds whole images of h x w slots with h and w from 4 to 14, numbered 0, 1, 2 in order from the row's start, followed by padding slots marked -1 (at least one in every row); some row holds the most images that fit.
All inputs are finite; a program needn't handle non-finite values.
Results may differ from a plain program's by a relative error of at most 0.013.
Values may be sent and summed in bfloat16 or wider, within the bound.
A program may use at most 256 MiB of HBM per device.

v0:
```python
import jax
import jax.numpy as jnp
from jax import lax
from jax.sharding import PartitionSpec as P

HEAD_DIM = 64


def layer_norm(values, gain, shift):
    center = values - jnp.mean(values, axis=-1, keepdims=True)
    spread = jnp.mean(center * center, axis=-1, keepdims=True)
    return center * lax.rsqrt(spread + 1e-06) * gain + shift


def gelu_exact(values):
    return jax.nn.gelu(values, approximate=False)


def masked_scores(queries, keys_row, segment_row):
    scores = (
        jnp.einsum("qhe,khe->hqk", queries, keys_row, preferred_element_type=jnp.float32) * 0.125
    )
    allowed = segment_row[:, None] == segment_row[None, :]
    return jnp.where(allowed[None], scores, -jnp.inf)


def row_forward(items):
    queries, keys_row, values_row, segment_row = items
    scores = masked_scores(queries, keys_row, segment_row)
    highest = jnp.max(scores, axis=-1, keepdims=True)
    expo = jnp.exp(scores - highest)
    totals = jnp.sum(expo, axis=-1, keepdims=True)
    probs = (expo / totals).astype(jnp.bfloat16)
    mixed = jnp.einsum("hqk,khe->qhe", probs, values_row, preferred_element_type=jnp.float32)
    return (mixed.astype(jnp.bfloat16), (highest + jnp.log(totals))[..., 0])


def row_backward(items):
    queries, keys_row, values_row, segment_row, grad_mixed, logsum = items
    scores = masked_scores(queries, keys_row, segment_row)
    probs = jnp.exp(scores - logsum[..., None])
    grad_probs = jnp.einsum(
        "qhe,khe->hqk", grad_mixed, values_row, preferred_element_type=jnp.float32
    )
    grad_values = jnp.einsum(
        "hqk,qhe->khe", probs.astype(jnp.bfloat16), grad_mixed, preferred_element_type=jnp.float32
    ).astype(jnp.bfloat16)
    inner = jnp.sum(probs * grad_probs, axis=-1, keepdims=True)
    grad_scores = (probs * (grad_probs - inner)).astype(jnp.bfloat16)
    grad_queries = (
        jnp.einsum("hqk,khe->qhe", grad_scores, keys_row, preferred_element_type=jnp.float32)
        * 0.125
    ).astype(jnp.bfloat16)
    grad_keys = (
        jnp.einsum("hqk,qhe->khe", grad_scores, queries, preferred_element_type=jnp.float32) * 0.125
    ).astype(jnp.bfloat16)
    return (grad_queries, grad_keys, grad_values)


def per_device(
    block_input,
    segment_ids,
    ln1_gain,
    ln1_bias,
    qkv_weight,
    qv_bias,
    out_weight,
    out_bias,
    ln2_gain,
    ln2_bias,
    up_weight,
    up_bias,
    down_weight,
    down_bias,
    out_cotangent,
):
    rows, slots, width = block_input.shape
    heads = width // HEAD_DIM
    shape_four = (rows, slots, heads, HEAD_DIM)
    attn_shards = (ln1_gain, ln1_bias, qkv_weight, qv_bias, out_weight, out_bias)
    mlp_shards = (ln2_gain, ln2_bias, up_weight, up_bias, down_weight, down_bias)
    attn_full = (
        lax.all_gather(attn_shards[0], "fsdp", axis=0, tiled=True),
        lax.all_gather(attn_shards[1], "fsdp", axis=0, tiled=True),
        lax.all_gather(attn_shards[2], "fsdp", axis=0, tiled=True),
        lax.all_gather(attn_shards[3], "fsdp", axis=0, tiled=True),
        lax.all_gather(attn_shards[4], "fsdp", axis=0, tiled=True),
        lax.all_gather(attn_shards[5], "fsdp", axis=0, tiled=True),
    )
    gain_one, shift_one, qkv_full, bias_full, proj_full, proj_bias = attn_full
    flat = block_input.reshape(-1, width).astype(jnp.float32)
    normed, norm_back = jax.vjp(
        layer_norm, flat, gain_one.astype(jnp.float32), shift_one.astype(jnp.float32)
    )
    normed_low = normed.astype(jnp.bfloat16)
    projected = jnp.dot(normed_low, qkv_full, preferred_element_type=jnp.float32)
    bias_wide = bias_full.astype(jnp.float32)
    queries = (projected[:, :width] + bias_wide[:width]).astype(jnp.bfloat16).reshape(shape_four)
    keys_all = projected[:, width : 2 * width].astype(jnp.bfloat16).reshape(shape_four)
    values_all = (
        (projected[:, 2 * width :] + bias_wide[width:]).astype(jnp.bfloat16).reshape(shape_four)
    )
    mixed, logsum = lax.map(row_forward, (queries, keys_all, values_all, segment_ids))
    mixed_flat = mixed.reshape(-1, width)
    middle = (
        flat
        + jnp.dot(mixed_flat, proj_full, preferred_element_type=jnp.float32)
        + proj_bias.astype(jnp.float32)
    )
    mlp_full = (
        lax.all_gather(mlp_shards[0], "fsdp", axis=0, tiled=True),
        lax.all_gather(mlp_shards[1], "fsdp", axis=0, tiled=True),
        lax.all_gather(mlp_shards[2], "fsdp", axis=0, tiled=True),
        lax.all_gather(mlp_shards[3], "fsdp", axis=0, tiled=True),
        lax.all_gather(mlp_shards[4], "fsdp", axis=0, tiled=True),
        lax.all_gather(mlp_shards[5], "fsdp", axis=0, tiled=True),
    )
    gain_two, shift_two, up_full, up_shift, down_full, down_shift = mlp_full
    normed_two, norm_two_back = jax.vjp(
        layer_norm, middle, gain_two.astype(jnp.float32), shift_two.astype(jnp.float32)
    )
    normed_two_low = normed_two.astype(jnp.bfloat16)
    hidden_pre = jnp.dot(
        normed_two_low, up_full, preferred_element_type=jnp.float32
    ) + up_shift.astype(jnp.float32)
    hidden_act, gelu_back = jax.vjp(gelu_exact, hidden_pre)
    hidden_low = hidden_act.astype(jnp.bfloat16)
    output = (
        middle
        + jnp.dot(hidden_low, down_full, preferred_element_type=jnp.float32)
        + down_shift.astype(jnp.float32)
    )
    block_output = output.astype(jnp.bfloat16).reshape(rows, slots, width)
    mlp_again = (
        lax.all_gather(mlp_shards[0], "fsdp", axis=0, tiled=True),
        lax.all_gather(mlp_shards[1], "fsdp", axis=0, tiled=True),
        lax.all_gather(mlp_shards[2], "fsdp", axis=0, tiled=True),
        lax.all_gather(mlp_shards[3], "fsdp", axis=0, tiled=True),
        lax.all_gather(mlp_shards[4], "fsdp", axis=0, tiled=True),
        lax.all_gather(mlp_shards[5], "fsdp", axis=0, tiled=True),
    )
    up_back = mlp_again[2]
    down_back = mlp_again[4]
    cotangent = out_cotangent.reshape(-1, width)
    cot_wide = cotangent.astype(jnp.float32)
    down_bias_grad = jnp.sum(cot_wide, axis=0)
    down_weight_grad = jnp.einsum(
        "nf,nd->fd", hidden_low, cotangent, preferred_element_type=jnp.float32
    )
    grad_hidden = jnp.einsum("nd,fd->nf", cotangent, down_back, preferred_element_type=jnp.float32)
    grad_pre = gelu_back(grad_hidden)[0].astype(jnp.bfloat16)
    up_bias_grad = jnp.sum(grad_pre.astype(jnp.float32), axis=0)
    up_weight_grad = jnp.einsum(
        "nd,nf->df", normed_two_low, grad_pre, preferred_element_type=jnp.float32
    )
    grad_normed_two = jnp.einsum("nf,df->nd", grad_pre, up_back, preferred_element_type=jnp.float32)
    grad_mid_norm, gain_two_grad, shift_two_grad = norm_two_back(grad_normed_two)
    grad_middle = cot_wide + grad_mid_norm
    mlp_local = (
        gain_two_grad,
        shift_two_grad,
        up_weight_grad,
        up_bias_grad,
        down_weight_grad,
        down_bias_grad,
    )
    mlp_owned = (
        lax.psum_scatter(mlp_local[0], "fsdp", scatter_dimension=0, tiled=True),
        lax.psum_scatter(mlp_local[1], "fsdp", scatter_dimension=0, tiled=True),
        lax.psum_scatter(mlp_local[2], "fsdp", scatter_dimension=0, tiled=True),
        lax.psum_scatter(mlp_local[3], "fsdp", scatter_dimension=0, tiled=True),
        lax.psum_scatter(mlp_local[4], "fsdp", scatter_dimension=0, tiled=True),
        lax.psum_scatter(mlp_local[5], "fsdp", scatter_dimension=0, tiled=True),
    )
    mlp_summed = (
        lax.psum(mlp_owned[0].astype(jnp.bfloat16), "dp").astype(jnp.float32),
        lax.psum(mlp_owned[1].astype(jnp.bfloat16), "dp").astype(jnp.float32),
        lax.psum(mlp_owned[2].astype(jnp.bfloat16), "dp").astype(jnp.float32),
        lax.psum(mlp_owned[3].astype(jnp.bfloat16), "dp").astype(jnp.float32),
        lax.psum(mlp_owned[4].astype(jnp.bfloat16), "dp").astype(jnp.float32),
        lax.psum(mlp_owned[5].astype(jnp.bfloat16), "dp").astype(jnp.float32),
    )
    attn_again = (
        lax.all_gather(attn_shards[0], "fsdp", axis=0, tiled=True),
        lax.all_gather(attn_shards[1], "fsdp", axis=0, tiled=True),
        lax.all_gather(attn_shards[2], "fsdp", axis=0, tiled=True),
        lax.all_gather(attn_shards[3], "fsdp", axis=0, tiled=True),
        lax.all_gather(attn_shards[4], "fsdp", axis=0, tiled=True),
        lax.all_gather(attn_shards[5], "fsdp", axis=0, tiled=True),
    )
    qkv_back = attn_again[2]
    proj_back = attn_again[4]
    grad_branch = grad_middle.astype(jnp.bfloat16)
    out_bias_grad = jnp.sum(grad_branch.astype(jnp.float32), axis=0)
    out_weight_grad = jnp.einsum(
        "nd,ne->de", mixed_flat, grad_branch, preferred_element_type=jnp.float32
    )
    grad_mixed = jnp.einsum(
        "ne,de->nd", grad_branch, proj_back, preferred_element_type=jnp.float32
    ).astype(jnp.bfloat16)
    grad_queries, grad_keys, grad_values = lax.map(
        row_backward,
        (queries, keys_all, values_all, segment_ids, grad_mixed.reshape(shape_four), logsum),
    )
    grad_queries = grad_queries.reshape(-1, width)
    grad_keys = grad_keys.reshape(-1, width)
    grad_values = grad_values.reshape(-1, width)
    grad_projected = jnp.concatenate([grad_queries, grad_keys, grad_values], axis=1)
    qv_bias_grad = jnp.concatenate(
        [
            jnp.sum(grad_queries.astype(jnp.float32), axis=0),
            jnp.sum(grad_values.astype(jnp.float32), axis=0),
        ]
    )
    qkv_weight_grad = jnp.einsum(
        "nd,nc->dc", normed_low, grad_projected, preferred_element_type=jnp.float32
    )
    grad_normed = jnp.einsum(
        "nc,dc->nd", grad_projected, qkv_back, preferred_element_type=jnp.float32
    )
    grad_flat_norm, gain_one_grad, shift_one_grad = norm_back(grad_normed)
    input_grad = (grad_middle + grad_flat_norm).astype(jnp.bfloat16).reshape(rows, slots, width)
    attn_local = (
        gain_one_grad,
        shift_one_grad,
        qkv_weight_grad,
        qv_bias_grad,
        out_weight_grad,
        out_bias_grad,
    )
    attn_owned = (
        lax.psum_scatter(attn_local[0], "fsdp", scatter_dimension=0, tiled=True),
        lax.psum_scatter(attn_local[1], "fsdp", scatter_dimension=0, tiled=True),
        lax.psum_scatter(attn_local[2], "fsdp", scatter_dimension=0, tiled=True),
        lax.psum_scatter(attn_local[3], "fsdp", scatter_dimension=0, tiled=True),
        lax.psum_scatter(attn_local[4], "fsdp", scatter_dimension=0, tiled=True),
        lax.psum_scatter(attn_local[5], "fsdp", scatter_dimension=0, tiled=True),
    )
    attn_summed = (
        lax.psum(attn_owned[0].astype(jnp.bfloat16), "dp").astype(jnp.float32),
        lax.psum(attn_owned[1].astype(jnp.bfloat16), "dp").astype(jnp.float32),
        lax.psum(attn_owned[2].astype(jnp.bfloat16), "dp").astype(jnp.float32),
        lax.psum(attn_owned[3].astype(jnp.bfloat16), "dp").astype(jnp.float32),
        lax.psum(attn_owned[4].astype(jnp.bfloat16), "dp").astype(jnp.float32),
        lax.psum(attn_owned[5].astype(jnp.bfloat16), "dp").astype(jnp.float32),
    )
    return (
        block_output,
        input_grad,
        attn_summed[0],
        attn_summed[1],
        attn_summed[2],
        attn_summed[3],
        attn_summed[4],
        attn_summed[5],
        mlp_summed[0],
        mlp_summed[1],
        mlp_summed[2],
        mlp_summed[3],
        mlp_summed[4],
        mlp_summed[5],
    )


def solution(mesh):
    return jax.shard_map(
        per_device,
        mesh=mesh,
        in_specs=(
            P(("fsdp", "dp"), None, None),
            P(("fsdp", "dp"), None),
            P("fsdp"),
            P("fsdp"),
            P("fsdp", None),
            P("fsdp"),
            P("fsdp", None),
            P("fsdp"),
            P("fsdp"),
            P("fsdp"),
            P("fsdp", None),
            P("fsdp"),
            P("fsdp", None),
            P("fsdp"),
            P(("fsdp", "dp"), None, None),
        ),
        out_specs=(
            P(("fsdp", "dp"), None, None),
            P(("fsdp", "dp"), None, None),
            P("fsdp"),
            P("fsdp"),
            P("fsdp", None),
            P("fsdp"),
            P("fsdp", None),
            P("fsdp"),
            P("fsdp"),
            P("fsdp"),
            P("fsdp", None),
            P("fsdp"),
            P("fsdp", None),
            P("fsdp"),
        ),
        check_vma=False,
    )
```

profile of v0, /device:TPU:0, one launch (start us, length us, event | category | flops | bytes accessed | tf_op | source)
XLA Modules:
  0.0 992.4 jit_solution(8717277212317786385)
XLA Ops:
  20.1 64.0 %all-reduce.17 = (bf16[768]{0:T(1024)(128)(2,1)S(1)}, bf16[768]{0:T(1024)(128)(2,1)S(1)}, bf16[1536]{0:T(1024)(128)(2,1)S(1)}, bf16[768]{0:T(1024)(128)(2,1)S(1)...) all-reduce(bf16[768]{0:T(1024)(128)(2,1)S(1)} %dynamic-update-slice, ...), channel_id=1, replica_groups=mesh['fsdp'=16,'dp'=2] {'fsdp'}, use_global_device_ids=true, to_apply=%add.1 | all-reduce | flops 9216 | bytes 36864
  91.7 10.9 %fusion.78 = f32[2080,2304]{1,0:T(8,128)S(1)} fusion(bf16[2080,768]{1,0:T(8,128)(2,1)} %get-tuple-element.243, bf16[768,2304]{1,0:T(8,128)(2,1)} %all-gather.5.cloned.1.call-done), kind=kOutput, calls=%fused_computation.139 | convolution fusion | flops 7361003520 | bytes 25903104 | tf_op jit(solution)/shard_map/dot_general | solution.py:96
  107.0 10.8 %reshape.303 = bf16[5,416,12,64]{3,2,1,0:T(8,128)(2,1)} reshape(bf16[2080,768]{1,0:T(8,128)(2,1)} %get-tuple-element.241) | data formatting | bytes 6389760 | tf_op jit(solution)/shard_map/reshape | solution.py:101
  117.8 10.7 %copy.66 = bf16[5,416,12,64]{1,3,2,0:T(8,128)(2,1)} copy(bf16[5,416,12,64]{3,2,1,0:T(8,128)(2,1)} %reshape.303) | data formatting | bytes 6389760 | tf_op jit(solution)/shard_map/while | solution.py:103
  136.1 10.8 %copy.67 = bf16[5,416,12,64]{1,3,2,0:T(8,128)(2,1)} copy(bf16[5,416,12,64]{3,2,1,0:T(8,128)(2,1)} %reshape.304) | data formatting | bytes 6389760 | tf_op jit(solution)/shard_map/while | solution.py:103
  155.1 10.7 %copy.68 = bf16[5,416,12,64]{1,3,2,0:T(8,128)(2,1)} copy(bf16[5,416,12,64]{3,2,1,0:T(8,128)(2,1)} %reshape.305) | data formatting | bytes 6389760 | tf_op jit(solution)/shard_map/while | solution.py:103
  168.1 59.9 %while.26 = (s32[]{:T(128)}, bf16[5,416,12,64]{1,3,2,0:T(8,128)(2,1)}, f32[5,12,416]{2,1,0:T(8,128)}, bf16[5,416,12,64]{1,3,2,0:T(8,128)(2,1)}, s32[5,416]{1,0:T...) while((s32[]{:T(128)}, bf16[5,416,12,64]{1,3,2,0:T(8,128)(2,1)}, ...), condition=%wide.region_5.6_spmd, body=%wide.region_2.5_spmd.sunk | while | flops 557035648 | bytes 28938200 | solution.py:103
  235.7 9.7 reshape.245
  260.6 71.5 %multiply_convert_fusion.3 = (bf16[2080,3072]{1,0:T(8,128)(2,1)}, f32[2080,3072]{1,0:T(8,128)}, f32[2080,3072]{1,0:T(8,128)}) fusion(f32[3072]{0:T(1024)S(1)} %copy-done.33, bf16[768,3072]{1,0:T(8,128)(2,1)} %all-gather.9.cloned.1.call-done, f32[2080,768]{1,0:T(8,128)} %fusion.67, f32[768]{0:T(1024)S(1)} %copy-done.35, f32[768]{0:T(1024)S(1)} %copy-done.30, ...), kind=kOutput, calls=%fused_computation.68 | convolution fusion | flops 10244382720 | bytes 75041024 | tf_op jit(solution)/shard_map/dot_general | solution.py:123
  332.1 28.3 %convert_reduce_fusion = (f32[3072]{0:T(1024)}, bf16[2080,3072]{1,0:T(8,128)(2,1)}) fusion(f32[2080,3072]{1,0:T(8,128)} %get-tuple-element.235, bf16[2080,768]{1,0:T(8,128)(2,1)S(1)} %bitcast.159, bf16[3072,768]{1,0:T(8,128)(2,1)} %all-gather.11.cloned.1.call-done, f32[2080,3072]{1,0:T(8,128)} %get-tuple-element.248, f32[3072]{0:T(1024)S(1)} %copy-done.33), kind=kOutput, calls=%fused_computation.66 | convolution fusion | flops 9923294208 | bytes 71835648 | tf_op jit(solution)/shard_map/nd,fd->nf/dot_general | solution.py:150
  360.5 22.1 %multiply_reduce_fusion.1 = (f32[768]{0:T(1024)}, f32[2080]{0:T(1024)S(1)}, f32[768]{0:T(1024)}, f32[2080,768]{1,0:T(8,128)}) fusion(f32[2080,768]{1,0:T(8,128)} %fusion.67, f32[2080]{0:T(1024)S(1)} %fusion.69, f32[2080]{0:T(1024)S(1)} %broadcast_multiply_fusion.1, f32[768]{0:T(1024)S(1)} %copy-done.30, bf16[2080,3072]{1,0:T(8,128)(2,1)} %get-tuple-element.252, ...), kind=kOutput, calls=%fused_computation.98 | convolution fusion | flops 9827446784 | bytes 30311808 | tf_op jit(solution)/shard_map/nf,df->nd/dot_general | solution.py:156
  402.7 10.8 %reshape.294 = bf16[5,416,12,64]{3,2,1,0:T(8,128)(2,1)} reshape(bf16[2080,768]{1,0:T(8,128)(2,1)} %convolution_convert_fusion) | data formatting | bytes 6389760 | tf_op jit(solution)/shard_map/reshape | solution.py:203
  413.5 10.7 %copy.73 = bf16[5,416,12,64]{1,3,2,0:T(8,128)(2,1)} copy(bf16[5,416,12,64]{3,2,1,0:T(8,128)(2,1)} %reshape.294) | data formatting | bytes 6389760 | tf_op jit(solution)/shard_map/while | solution.py:201
  431.4 121.2 %while.27 = (s32[]{:T(128)}, bf16[5,416,12,64]{1,3,2,0:T(8,128)(2,1)}, bf16[5,416,12,64]{1,3,2,0:T(8,128)(2,1)}, bf16[5,416,12,64]{1,3,2,0:T(8,128)(2,1)}, bf16[...) while((s32[]{:T(128)}, ...), condition=%wide.region_12.13_spmd, body=%wide.region_10.12_spmd.sunk | while | flops 1361985664 | bytes 71006704 | solution.py:201
  576.5 9.5 reshape.250
  610.5 11.0 %fusion.79 = f32[768,2304]{1,0:T(8,128)} fusion(bf16[2080,768]{1,0:T(8,128)(2,1)S(1)} %copy-done.12, bf16[2080,2304]{0,1:T(8,128)(2,1)S(1)} %constant_dynamic-update-slice_fusion), kind=kOutput, calls=%fused_computation.140 | convolution fusion | flops 7361003520 | bytes 19857408 | tf_op jit(solution)/shard_map/nd,nc->dc/dot_general | solution.py:215
  622.3 19.4 %fusion.70 = f32[768,3072]{1,0:T(8,128)} fusion(bf16[2080,3072]{1,0:T(8,128)(2,1)} %get-tuple-element.252, f32[2080,768]{1,0:T(8,128)} %fusion.67, f32[768]{0:T(1024)S(1)} %copy-done.36, f32[768]{0:T(1024)S(1)} %copy-done.31, f32[2080]{0:T(1024)S(1)} %copy-done.27, f32[2080]{0:T(1024)S(1)} %copy-done.21), kind=kOutput, calls=%fused_computation.133 | convolution fusion | flops 9822658560 | bytes 28629248 | tf_op jit(solution)/shard_map/nd,nf->df/dot_general | solution.py:153
  643.6 15.7 %fusion.81 = f32[3072,768]{1,0:T(8,128)} fusion(bf16[2080,3072]{1,0:T(8,128)(2,1)} %get-tuple-element.234, bf16[2080,768]{1,0:T(8,128)(2,1)S(1)} %bitcast.160), kind=kOutput, calls=%fused_computation.142 | convolution fusion | flops 9814671360 | bytes 25411584 | tf_op jit(solution)/shard_map/nf,nd->fd/dot_general | solution.py:147
  668.9 19.5 %fusion.72 = (f32[768]{0:T(1024)S(1)}, f32[2080]{0:T(1024)S(1)}, f32[768]{0:T(1024)S(1)}, f32[2080,768]{1,0:T(8,128)}) fusion(f32[2080,768]{1,0:T(8,128)} %get-tuple-element.242, f32[768]{0:T(1024)S(1)} %copy-done.29, f32[2080]{0:T(1024)S(1)} %copy-done.17, f32[2080]{0:T(1024)S(1)} %copy-done.15, bf16[5,416,768]{2,1,0:T(8,128)(2,1)S(1)} %copy-done.4, ...), kind=kOutput, calls=%fused_computation.135 | convolution fusion | flops 7375376384 | bytes 29132160 | tf_op jit(solution)/shard_map/nc,dc->nd/dot_general | solution.py:218
  688.7 58.4 %all-reduce.16 = (bf16[768]{0:T(1024)(128)(2,1)S(1)}, bf16[768]{0:T(1024)(128)(2,1)S(1)}, bf16[1536]{0:T(1024)(128)(2,1)S(1)}, bf16[768]{0:T(1024)(128)(2,1)S(1)...) all-reduce(f32[768]{0:T(1024)S(1)} %get-tuple-element.167, ...), channel_id=2, replica_groups=mesh['fsdp'=16,'dp'=2] {'fsdp'}, use_global_device_ids=true, to_apply=%region_16.17.clone | all-reduce | flops 9216 | bytes 55296
  767.2 16.9 %add_convert_fusion.2 = bf16[2080,768]{1,0:T(8,128)(2,1)} fusion(f32[2080,768]{1,0:T(8,128)} %fusion.67, bf16[2080,3072]{1,0:T(8,128)(2,1)} %get-tuple-element.234, bf16[3072,768]{1,0:T(8,128)(2,1)} %all-gather.11.cloned.1.call-done, f32[768]{0:T(1024)S(1)} %convert_element_type.205), kind=kOutput, calls=%fused_computation.105 | convolution fusion | flops 9819463680 | bytes 27085824 | tf_op jit(solution)/shard_map/dot_general | solution.py:130
  787.4 36.4 %reduce-scatter.9.cloned.1.call-done = f32[48,3072]{1,0:T(8,128)} async-done(((f32[768,3072]{1,0:T(8,128)}), f32[48,3072]{1,0:T(8,128)}) %reduce-scatter.9.cloned.1.call-update) | async-done | bytes 589840 | tf_op jit(solution)/shard_map/reduce_scatter | solution.py:170
  825.6 113.2 %reduce-scatter.11.cloned.1.call-done = f32[192,768]{1,0:T(8,128)} async-done(((f32[3072,768]{1,0:T(8,128)}), f32[192,768]{1,0:T(8,128)}) %reduce-scatter.11.cloned.1.call-update) | async-done | bytes 589840 | tf_op jit(solution)/shard_map/reduce_scatter | solution.py:172
  947.6 31.1 %all-reduce.22.cloned.1.call-done = (bf16[48,2304]{1,0:T(8,128)(2,1)}, bf16[48,768]{1,0:T(8,128)(2,1)}, bf16[48,3072]{1,0:T(8,128)(2,1)}, bf16[192,768]{1,0:T(8,128)(2,1)}) async-done(((bf16[48,2304]{1,0:T(8,128)(2,1)}, bf16[48,768]{1,0:T(8,128)(2,1)}, bf16[48,3072]{1,0:T(8,128)(2,1)}, bf16[192,768]{1,0:T(8,128)(2,1)}), (bf16[48,2304]{1,0:T(8,128)(2,1)}, bf16[48,768]{1,0:T(8,128)(2,1)}, ...) | async-done | bytes 884752 | tf_op jit(solution)/shard_map/psum | solution.py:242
  (296 shorter events, 370.9 us)
Async XLA Ops:
  7.2 79.5 %copy-start.2 = (bf16[5,416,768]{2,1,0:T(8,128)(2,1)S(1)}, bf16[5,416,768]{2,1,0:T(8,128)(2,1)}, u32[]{:S(2)}) copy-start(bf16[5,416,768]{2,1,0:T(8,128)(2,1)} %param.19) | copy-start | bytes 9584644
  7.3 12.6 %copy-start.49 = (bf16[96]{0:T(256)(128)(2,1)S(1)}, bf16[96]{0:T(256)(128)(2,1)}, u32[]{:S(2)}) copy-start(bf16[96]{0:T(256)(128)(2,1)} %param.24) | copy-start | bytes 580
  7.3 84.4 %all-gather.5.cloned.1.call-start = ((), (), s32[]{:S(2)}) async-start(), calls=%async_computation.4 | async-start | bytes 3760128 | tf_op jit(solution)/shard_map/all_gather | solution.py:85
  8.0 237.3 %all-gather.7.cloned.1.call-start = ((), (), s32[]{:S(2)}) async-start(), calls=%async_computation.5 | async-start | bytes 1253376 | tf_op jit(solution)/shard_map/all_gather | solution.py:87
  8.8 251.8 %all-gather.9.cloned.1.call-start = ((), (), s32[]{:S(2)}) async-start(), calls=%async_computation.6 | async-start | bytes 5013504 | tf_op jit(solution)/shard_map/all_gather | solution.py:113
  9.5 322.6 %all-gather.11.cloned.1.call-start = ((), (), s32[]{:S(2)}) async-start(), calls=%async_computation.7 | async-start | bytes 5013504 | tf_op jit(solution)/shard_map/all_gather | solution.py:115
  10.1 774.1 %reduce-scatter.7.cloned.1.call-start = ((), (), s32[]{:S(2)}) async-start(), calls=%async_computation.9 | async-start | bytes 2506752 | tf_op jit(solution)/shard_map/reduce_scatter | solution.py:236
  15.6 76.1 %copy-start.14 = (f32[2080]{0:T(1024)}, f32[2080]{0:T(1024)S(1)}, u32[]{:S(2)}) copy-start(f32[2080]{0:T(1024)S(1)} %div.47) | copy-start | bytes 24964
  256.3 126.3 %copy-start.20 = (f32[2080]{0:T(1024)}, f32[2080]{0:T(1024)S(1)}, u32[]{:S(2)}) copy-start(f32[2080]{0:T(1024)S(1)} %broadcast_multiply_fusion.1) | copy-start | bytes 24964
  260.6 122.0 %copy-start.26 = (f32[2080]{0:T(1024)}, f32[2080]{0:T(1024)S(1)}, u32[]{:S(2)}) copy-start(f32[2080]{0:T(1024)S(1)} %fusion.69) | copy-start | bytes 24964
  260.6 71.5 %copy-start.5 = (bf16[5,416,768]{2,1,0:T(8,128)(2,1)S(1)}, bf16[5,416,768]{2,1,0:T(8,128)(2,1)}, u32[]{:S(2)}) copy-start(bf16[5,416,768]{2,1,0:T(8,128)(2,1)} %param.33) | copy-start | bytes 9584644
  360.5 22.1 %copy-start.23 = (f32[2080]{0:T(1024)S(1)}, f32[2080]{0:T(1024)}, u32[]{:S(2)}) copy-start(f32[2080]{0:T(1024)} %copy-done.22) | copy-start | bytes 24964
  360.5 22.1 %copy-start.1 = (f32[2080,768]{1,0:T(8,128)S(1)}, f32[2080,768]{1,0:T(8,128)}, u32[]{:S(2)}) copy-start(f32[2080,768]{1,0:T(8,128)} %fusion.67) | copy-start | bytes 19169284
  424.2 361.5 %reduce-scatter.5.cloned.1.call-start = ((), (), s32[]{:S(2)}) async-start(), calls=%async_computation.8 | async-start | bytes 7520256 | tf_op jit(solution)/shard_map/reduce_scatter | solution.py:234
  621.6 202.2 %reduce-scatter.9.cloned.1.call-start = ((), (), s32[]{:S(2)}) async-start(), calls=%async_computation.10 | async-start | bytes 10027008 | tf_op jit(solution)/shard_map/reduce_scatter | solution.py:170
  641.7 297.1 %reduce-scatter.11.cloned.1.call-start = ((), (), s32[]{:S(2)}) async-start(), calls=%async_computation.11 | async-start | bytes 10027008 | tf_op jit(solution)/shard_map/reduce_scatter | solution.py:172
  659.4 319.4 %all-reduce.22.cloned.1.call-start = ((), (), s32[]{:S(2)}) async-start(), calls=%async_computation.12 | async-start | bytes 1769472 | tf_op jit(solution)/shard_map/psum | solution.py:242
  668.9 19.6 %copy-start.32 = (f32[768]{0:T(1024)S(1)}, f32[768]{0:T(1024)}, u32[]{:S(2)}) copy-start(f32[768]{0:T(1024)} %get-tuple-element.230) | copy-start | bytes 9220
  668.9 19.6 %copy-start.34 = (f32[3072]{0:T(1024)S(1)}, f32[3072]{0:T(1024)}, u32[]{:S(2)}) copy-start(f32[3072]{0:T(1024)} %get-tuple-element.251) | copy-start | bytes 36868
  668.9 19.6 %copy-start.38 = (f32[768]{0:T(1024)S(1)}, f32[768]{0:T(1024)}, u32[]{:S(2)}) copy-start(f32[768]{0:T(1024)} %get-tuple-element.162) | copy-start | bytes 9220
  668.9 19.6 %copy-start.39 = (f32[768]{0:T(1024)S(1)}, f32[768]{0:T(1024)}, u32[]{:S(2)}) copy-start(f32[768]{0:T(1024)} %get-tuple-element.164) | copy-start | bytes 9220
  668.9 87.8 %copy-start.25 = (f32[2080]{0:T(1024)S(1)}, f32[2080]{0:T(1024)}, u32[]{:S(2)}) copy-start(f32[2080]{0:T(1024)} %copy-done.24) | copy-start | bytes 24964
  767.2 173.5 %copy-start.7 = (bf16[5,416,768]{2,1,0:T(8,128)(2,1)S(1)}, bf16[5,416,768]{2,1,0:T(8,128)(2,1)}, u32[]{:S(2)}) copy-start(bf16[5,416,768]{2,1,0:T(8,128)(2,1)} %param.33) | copy-start | bytes 9584644
  767.2 173.5 %copy-start.19 = (f32[2080]{0:T(1024)S(1)}, f32[2080]{0:T(1024)}, u32[]{:S(2)}) copy-start(f32[2080]{0:T(1024)} %copy-done.18) | copy-start | bytes 24964
  (35 other events, 241.9 us)
Sparse Core Ops, SparseCore 0:
  10.4 50.3 all-gather.4
  63.1 36.6 all-gather.6
  102.1 51.9 all-gather.8
  156.3 51.6 all-gather.10
  424.3 60.4 reduce-scatter.6
  621.7 87.2 reduce-scatter.4
  713.1 110.7 reduce-scatter.8
  827.9 110.8 reduce-scatter.10
  942.5 36.2 all-reduce.21
where the time goes:
time: 1000 us; the launch traced here: 992 us
  matrix products  370 us (37%)
  local copies, waits for them, and re-layouts  185 us (18%)
  waiting for transfers between devices  183 us (18%)
  blocking collectives  127 us (13%)
  other arithmetic  107 us (11%)
  between operations  18.9 us (2%)
    unnamed x2, blocking collectives  122 us
    reduce_scatter x1, waiting for transfers between devices, per_device(): lax.psum_scatter(mlp_local[4], 'fsdp', scatter_dimension=0, tiled=True)  113 us
    dot_general x1, matrix products, per_device(): jnp.dot(normed_two_low, up_full, preferred_element_type=jnp.float32)  71.5 us
    while x4, local copies, waits for them, and re-layouts, per_device(): lax.map(row_forward, (queries, keys_all, values_all, segment_ids))  39.8 us
    reduce_scatter x1, waiting for transfers between devices, per_device(): lax.psum_scatter(mlp_local[2], 'fsdp', scatter_dimension=0, tiled=True)  36.4 us
    while x4, local copies, waits for them, and re-layouts, per_device(): lax.map(row_backward, (queries, keys_all, values_all, segment_ids, grad_m...  33.9 us
    psum x1, waiting for transfers between devices, per_device(): lax.psum(attn_owned[2].astype(jnp.bfloat16), 'dp').astype(jnp.float32)  31.1 us
    dot_general x10, matrix products, masked_scores(): jnp.einsum('qhe,khe->hqk', queries, keys_row, preferred_element_type=jnp....  31.1 us
  transfers between devices with their start and end apart: 9, of which 3 were waited for; matrix products, arithmetic and copies ran while one was open for 56% of the time, Pallas kernels for 0%

commit v1 on v0

--- a/solution.py
+++ b/solution.py
@@ -239,7 +239,9 @@
     attn_summed = (
         lax.psum(attn_owned[0].astype(jnp.bfloat16), "dp").astype(jnp.float32),
         lax.psum(attn_owned[1].astype(jnp.bfloat16), "dp").astype(jnp.float32),
-        lax.psum(attn_owned[2].astype(jnp.bfloat16), "dp").astype(jnp.float32),
+        jnp.sum(lax.all_gather(attn_owned[2].astype(jnp.bfloat16), "dp"), axis=0).astype(
+            jnp.float32
+        ),
         lax.psum(attn_owned[3].astype(jnp.bfloat16), "dp").astype(jnp.float32),
         lax.psum(attn_owned[4].astype(jnp.bfloat16), "dp").astype(jnp.float32),
         lax.psum(attn_owned[5].astype(jnp.bfloat16), "dp").astype(jnp.float32),

time: 1000 us -> 841 us (0.84)
  waiting for transfers between devices: 183 us -> 19.2 us
  blocking collectives: 127 us -> 139 us
    reduce_scatter x1, waiting for transfers between devices: 113 us -> 0.01 us  [per_device(): lax.psum_scatter(mlp_local[4], 'fsdp', scatter_dimension=0, tiled=True)]
    reduce_scatter x1, waiting for transfers between devices: 36.4 us -> 0.01 us  [per_device(): lax.psum_scatter(mlp_local[2], 'fsdp', scatter_dimension=0, tiled=True)]
    psum x1, waiting for transfers between devices: 31.1 us -> 16.4 us  [per_device(): lax.psum(attn_owned[4].astype(jnp.bfloat16), 'dp').astype(jnp.float32)]
  transfers between devices with their start and end apart: 9 -> 9, of which waited for: 3 -> 1; matrix products, arithmetic and copies ran while one was open for 56% -> 69% of each run, Pallas kernels for 0% -> 0%
where the time goes in v1:
time: 841 us; the launch traced here: 833 us
  matrix products  367 us (44%)
  local copies, waits for them, and re-layouts  183 us (22%)
  blocking collectives  139 us (17%)
  other arithmetic  104 us (12%)
  waiting for transfers between devices  19.2 us (2%)
  between operations  18.9 us (2%)
    unnamed x2, blocking collectives  124 us
    dot_general x1, matrix products, per_device(): jnp.dot(normed_two_low, up_full, preferred_element_type=jnp.float32)  71.4 us
    while x4, local copies, waits for them, and re-layouts, per_device(): lax.map(row_forward, (queries, keys_all, values_all, segment_ids))  39.8 us
    while x4, local copies, waits for them, and re-layouts, per_device(): lax.map(row_backward, (queries, keys_all, values_all, segment_ids, grad_m...  34.5 us
    dot_general x10, matrix products, masked_scores(): jnp.einsum('qhe,khe->hqk', queries, keys_row, preferred_element_type=jnp....  31.1 us
    dot_general x1, matrix products, per_device(): jnp.einsum('nd,fd->nf', cotangent, down_back, preferred_element_type=jnp....  28.4 us
    dot_general x5, matrix products, row_backward(): jnp.einsum('qhe,khe->hqk', grad_mixed, values_row, preferred_element_type...  24.9 us
    dot_general x5, matrix products, row_forward(): jnp.einsum('hqk,khe->qhe', probs, values_row, preferred_element_type=jnp....  24.8 us
  transfers between devices with their start and end apart: 9, of which 1 were waited for; matrix products, arithmetic and copies ran while one was open for 69% of the time, Pallas kernels for 0%

profile of v1, /device:TPU:0, one launch (start us, length us, event | category | flops | bytes accessed | tf_op | source)
XLA Modules:
  0.0 832.6 jit_solution(475523369117711037)
XLA Ops:
  20.1 64.0 %all-reduce.17 = (bf16[768]{0:T(1024)(128)(2,1)S(1)}, bf16[768]{0:T(1024)(128)(2,1)S(1)}, bf16[1536]{0:T(1024)(128)(2,1)S(1)}, bf16[768]{0:T(1024)(128)(2,1)S(1)...) all-reduce(bf16[768]{0:T(1024)(128)(2,1)S(1)} %dynamic-update-slice, ...), channel_id=1, replica_groups=mesh['fsdp'=16,'dp'=2] {'fsdp'}, use_global_device_ids=true, to_apply=%add.1 | all-reduce | flops 9216 | bytes 36864
  91.7 10.9 %fusion.78 = f32[2080,2304]{1,0:T(8,128)S(1)} fusion(bf16[2080,768]{1,0:T(8,128)(2,1)} %get-tuple-element.242, bf16[768,2304]{1,0:T(8,128)(2,1)} %all-gather.6.cloned.1.call-done), kind=kOutput, calls=%fused_computation.139 | convolution fusion | flops 7361003520 | bytes 25903104 | tf_op jit(solution)/shard_map/dot_general | solution.py:96
  106.9 10.8 %reshape.304 = bf16[5,416,12,64]{3,2,1,0:T(8,128)(2,1)} reshape(bf16[2080,768]{1,0:T(8,128)(2,1)} %get-tuple-element.240) | data formatting | bytes 6389760 | tf_op jit(solution)/shard_map/reshape | solution.py:101
  117.8 10.6 %copy.66 = bf16[5,416,12,64]{1,3,2,0:T(8,128)(2,1)} copy(bf16[5,416,12,64]{3,2,1,0:T(8,128)(2,1)} %reshape.304) | data formatting | bytes 6389760 | tf_op jit(solution)/shard_map/while | solution.py:103
  136.1 10.8 %copy.67 = bf16[5,416,12,64]{1,3,2,0:T(8,128)(2,1)} copy(bf16[5,416,12,64]{3,2,1,0:T(8,128)(2,1)} %reshape.305) | data formatting | bytes 6389760 | tf_op jit(solution)/shard_map/while | solution.py:103
  155.0 10.7 %copy.68 = bf16[5,416,12,64]{1,3,2,0:T(8,128)(2,1)} copy(bf16[5,416,12,64]{3,2,1,0:T(8,128)(2,1)} %reshape.306) | data formatting | bytes 6389760 | tf_op jit(solution)/shard_map/while | solution.py:103
  168.1 59.9 %while.26 = (s32[]{:T(128)}, bf16[5,416,12,64]{1,3,2,0:T(8,128)(2,1)}, f32[5,12,416]{2,1,0:T(8,128)}, bf16[5,416,12,64]{1,3,2,0:T(8,128)(2,1)}, s32[5,416]{1,0:T...) while((s32[]{:T(128)}, bf16[5,416,12,64]{1,3,2,0:T(8,128)(2,1)}, ...), condition=%wide.region_5.6_spmd, body=%wide.region_2.5_spmd.sunk | while | flops 557035648 | bytes 28938200 | solution.py:103
  235.8 9.6 %reshape.245 = bf16[2080,768]{0,1:T(8,128)(2,1)} reshape(bf16[5,416,12,64]{1,0,3,2:T(8,128)(2,1)} %copy.69) | data formatting | bytes 6389760 | tf_op jit(solution)/shard_map/reshape | solution.py:104
  260.6 71.4 %multiply_convert_fusion.3 = (bf16[2080,3072]{1,0:T(8,128)(2,1)}, f32[2080,3072]{1,0:T(8,128)}, f32[2080,3072]{1,0:T(8,128)}) fusion(f32[3072]{0:T(1024)S(1)} %copy-done.27, bf16[768,3072]{1,0:T(8,128)(2,1)} %all-gather.10.cloned.1.call-done, f32[2080,768]{1,0:T(8,128)} %fusion.67, f32[768]{0:T(1024)S(1)} %copy-done.29, f32[768]{0:T(1024)S(1)} %copy-done.25, ...), kind=kOutput, calls=%fused_computation.68 | convolution fusion | flops 10244382720 | bytes 75041024 | tf_op jit(solution)/shard_map/dot_general | solution.py:123
  332.1 28.4 %convert_reduce_fusion = (f32[3072]{0:T(1024)}, bf16[2080,3072]{1,0:T(8,128)(2,1)}) fusion(f32[2080,3072]{1,0:T(8,128)} %get-tuple-element.234, bf16[2080,768]{1,0:T(8,128)(2,1)S(1)} %bitcast.162, bf16[3072,768]{1,0:T(8,128)(2,1)} %all-gather.12.cloned.1.call-done, f32[2080,3072]{1,0:T(8,128)} %get-tuple-element.247, f32[3072]{0:T(1024)S(1)} %copy-done.27), kind=kOutput, calls=%fused_computation.66 | convolution fusion | flops 9923294208 | bytes 71835648 | tf_op jit(solution)/shard_map/nd,fd->nf/dot_general | solution.py:150
  360.5 22.0 %multiply_reduce_fusion.1 = (f32[768]{0:T(1024)}, f32[2080]{0:T(1024)S(1)}, f32[768]{0:T(1024)}, f32[2080,768]{1,0:T(8,128)}) fusion(f32[2080,768]{1,0:T(8,128)} %fusion.67, f32[2080]{0:T(1024)S(1)} %fusion.69, f32[2080]{0:T(1024)S(1)} %broadcast_multiply_fusion.1, f32[768]{0:T(1024)S(1)} %copy-done.25, bf16[2080,3072]{1,0:T(8,128)(2,1)} %get-tuple-element.251, ...), kind=kOutput, calls=%fused_computation.98 | convolution fusion | flops 9827446784 | bytes 30311808 | tf_op jit(solution)/shard_map/nf,df->nd/dot_general | solution.py:156
  397.6 19.0 %fusion.70 = f32[768,3072]{1,0:T(8,128)} fusion(bf16[2080,3072]{1,0:T(8,128)(2,1)} %get-tuple-element.251, f32[2080,768]{1,0:T(8,128)} %fusion.67, f32[768]{0:T(1024)S(1)} %copy-done.29, f32[768]{0:T(1024)S(1)} %copy-done.25, f32[2080]{0:T(1024)S(1)} %fusion.69, f32[2080]{0:T(1024)S(1)} %broadcast_multiply_fusion.1), kind=kOutput, calls=%fused_computation.133 | convolution fusion | flops 9822658560 | bytes 28629248 | tf_op jit(solution)/shard_map/nd,nf->df/dot_general | solution.py:153
  422.0 10.8 %reshape.295 = bf16[5,416,12,64]{3,2,1,0:T(8,128)(2,1)} reshape(bf16[2080,768]{1,0:T(8,128)(2,1)} %convolution_convert_fusion) | data formatting | bytes 6389760 | tf_op jit(solution)/shard_map/reshape | solution.py:203
  432.8 10.8 %copy.73 = bf16[5,416,12,64]{1,3,2,0:T(8,128)(2,1)} copy(bf16[5,416,12,64]{3,2,1,0:T(8,128)(2,1)} %reshape.295) | data formatting | bytes 6389760 | tf_op jit(solution)/shard_map/while | solution.py:201
  443.6 15.9 %fusion.81 = f32[3072,768]{1,0:T(8,128)} fusion(bf16[2080,3072]{1,0:T(8,128)(2,1)} %get-tuple-element.233, bf16[2080,768]{1,0:T(8,128)(2,1)S(1)} %bitcast.163), kind=kOutput, calls=%fused_computation.142 | convolution fusion | flops 9814671360 | bytes 25411584 | tf_op jit(solution)/shard_map/nf,nd->fd/dot_general | solution.py:147
  466.6 121.9 %while.27 = (s32[]{:T(128)}, bf16[5,416,12,64]{1,3,2,0:T(8,128)(2,1)}, bf16[5,416,12,64]{1,3,2,0:T(8,128)(2,1)}, bf16[5,416,12,64]{1,3,2,0:T(8,128)(2,1)}, bf16[...) while((s32[]{:T(128)}, ...), condition=%wide.region_12.13_spmd, body=%wide.region_10.12_spmd.sunk | while | flops 1361985664 | bytes 71006704 | solution.py:201
  613.0 9.5 %reshape.250 = bf16[2080,768]{0,1:T(8,128)(2,1)} reshape(bf16[5,416,12,64]{1,0,3,2:T(8,128)(2,1)} %copy.76) | data formatting | bytes 6389760 | tf_op jit(solution)/shard_map/reshape | solution.py:206
  630.2 9.5 %reshape.251 = bf16[2080,768]{0,1:T(8,128)(2,1)} reshape(bf16[5,416,12,64]{1,0,3,2:T(8,128)(2,1)} %copy.77) | data formatting | bytes 6389760 | tf_op jit(solution)/shard_map/reshape | solution.py:207
  647.1 10.6 %fusion.79 = f32[768,2304]{1,0:T(8,128)} fusion(bf16[2080,768]{1,0:T(8,128)(2,1)S(1)} %copy-done.11, bf16[2080,2304]{0,1:T(8,128)(2,1)S(1)} %constant_dynamic-update-slice_fusion), kind=kOutput, calls=%fused_computation.140 | convolution fusion | flops 7361003520 | bytes 19857408 | tf_op jit(solution)/shard_map/nd,nc->dc/dot_general | solution.py:215
  662.6 17.1 %fusion.72 = (f32[768]{0:T(1024)S(1)}, f32[2080]{0:T(1024)S(1)}, f32[768]{0:T(1024)S(1)}, f32[2080,768]{1,0:T(8,128)S(1)}) fusion(f32[2080,768]{1,0:T(8,128)} %get-tuple-element.241, f32[768]{0:T(1024)S(1)} %copy-done.24, f32[2080]{0:T(1024)S(1)} %copy-done.16, f32[2080]{0:T(1024)S(1)} %copy-done.14, bf16[5,416,768]{2,1,0:T(8,128)(2,1)S(1)} %copy-done.4, ...), kind=kOutput, calls=%fused_computation.135 | convolution fusion | flops 7375376384 | bytes 29132160 | tf_op jit(solution)/shard_map/nc,dc->nd/dot_general | solution.py:218
  695.9 16.4 %add_convert_fusion.2 = bf16[2080,768]{1,0:T(8,128)(2,1)} fusion(f32[2080,768]{1,0:T(8,128)S(1)} %bitcast.161, bf16[2080,3072]{1,0:T(8,128)(2,1)} %get-tuple-element.233, bf16[3072,768]{1,0:T(8,128)(2,1)} %all-gather.12.cloned.1.call-done, f32[768]{0:T(1024)S(1)} %convert_element_type.207), kind=kOutput, calls=%fused_computation.105 | convolution fusion | flops 9819463680 | bytes 27085824 | tf_op jit(solution)/shard_map/dot_general | solution.py:130
  722.3 60.4 %all-reduce.16 = (bf16[768]{0:T(1024)(128)(2,1)S(1)}, bf16[768]{0:T(1024)(128)(2,1)S(1)}, bf16[1536]{0:T(1024)(128)(2,1)S(1)}, bf16[768]{0:T(1024)(128)(2,1)S(1)...) all-reduce(f32[768]{0:T(1024)S(1)} %get-tuple-element.167, ...), channel_id=3, replica_groups=mesh['fsdp'=16,'dp'=2] {'fsdp'}, use_global_device_ids=true, to_apply=%region_16.17.clone | all-reduce | flops 9216 | bytes 55296
  793.4 9.7 %all-gather = bf16[96,2304]{1,0:T(8,128)(2,1)S(1)} all-gather(bf16[48,2304]{1,0:T(8,128)(2,1)S(1)} %convert_element_type.218), channel_id=2, replica_groups=mesh['fsdp'=16,'dp'=2] {'dp'}, dimensions={0}, use_global_device_ids=true | all-gather | bytes 663552 | tf_op jit(solution)/shard_map/all_gather | solution.py:242
  804.1 16.4 %all-reduce.22.cloned.1.call-done = (bf16[48,768]{1,0:T(8,128)(2,1)}, bf16[48,3072]{1,0:T(8,128)(2,1)}, bf16[192,768]{1,0:T(8,128)(2,1)}) async-done(((bf16[48,768]{1,0:T(8,128)(2,1)}, bf16[48,3072]{1,0:T(8,128)(2,1)}, bf16[192,768]{1,0:T(8,128)(2,1)}), (bf16[48,768]{1,0:T(8,128)(2,1)}, bf16[48,3072]{1,0:T(8,128)(2,1)}, bf16[192,768]{1,0:T(8,128)(2,1)})) %all-reduce.22.cloned.1.call-update) | async-done | bytes 663568 | tf_op jit(solution)/shard_map/psum | solution.py:246
  (289 shorter events, 357.6 us)
Async XLA Ops:
  7.2 79.5 %copy-start.2 = (bf16[5,416,768]{2,1,0:T(8,128)(2,1)S(1)}, bf16[5,416,768]{2,1,0:T(8,128)(2,1)}, u32[]{:S(2)}) copy-start(bf16[5,416,768]{2,1,0:T(8,128)(2,1)} %param.19) | copy-start | bytes 9584644
  7.2 11.0 %copy-start.35 = (bf16[48]{0:T(256)(128)(2,1)S(1)}, bf16[48]{0:T(256)(128)(2,1)}, u32[]{:S(2)}) copy-start(bf16[48]{0:T(256)(128)(2,1)} %param.21) | copy-start | bytes 292
  7.2 11.2 %copy-start.36 = (bf16[48]{0:T(256)(128)(2,1)S(1)}, bf16[48]{0:T(256)(128)(2,1)}, u32[]{:S(2)}) copy-start(bf16[48]{0:T(256)(128)(2,1)} %param.22) | copy-start | bytes 292
  7.2 11.5 %copy-start.37 = (bf16[48]{0:T(256)(128)(2,1)S(1)}, bf16[48]{0:T(256)(128)(2,1)}, u32[]{:S(2)}) copy-start(bf16[48]{0:T(256)(128)(2,1)} %param.26) | copy-start | bytes 292
  7.2 11.7 %copy-start.38 = (bf16[48]{0:T(256)(128)(2,1)S(1)}, bf16[48]{0:T(256)(128)(2,1)}, u32[]{:S(2)}) copy-start(bf16[48]{0:T(256)(128)(2,1)} %param.27) | copy-start | bytes 292
  7.2 11.9 %copy-start.39 = (bf16[48]{0:T(256)(128)(2,1)S(1)}, bf16[48]{0:T(256)(128)(2,1)}, u32[]{:S(2)}) copy-start(bf16[48]{0:T(256)(128)(2,1)} %param.28) | copy-start | bytes 292
  7.3 12.1 %copy-start.40 = (bf16[48]{0:T(256)(128)(2,1)S(1)}, bf16[48]{0:T(256)(128)(2,1)}, u32[]{:S(2)}) copy-start(bf16[48]{0:T(256)(128)(2,1)} %param.32) | copy-start | bytes 292
  7.3 12.4 %copy-start.41 = (bf16[192]{0:T(256)(128)(2,1)S(1)}, bf16[192]{0:T(256)(128)(2,1)}, u32[]{:S(2)}) copy-start(bf16[192]{0:T(256)(128)(2,1)} %param.30) | copy-start | bytes 1156
  7.3 12.6 %copy-start.42 = (bf16[96]{0:T(256)(128)(2,1)S(1)}, bf16[96]{0:T(256)(128)(2,1)}, u32[]{:S(2)}) copy-start(bf16[96]{0:T(256)(128)(2,1)} %param.24) | copy-start | bytes 580
  7.3 84.4 %all-gather.6.cloned.1.call-start = ((), (), s32[]{:S(2)}) async-start(), calls=%async_computation.4 | async-start | bytes 3760128 | tf_op jit(solution)/shard_map/all_gather | solution.py:85
  8.0 237.4 %all-gather.8.cloned.1.call-start = ((), (), s32[]{:S(2)}) async-start(), calls=%async_computation.5 | async-start | bytes 1253376 | tf_op jit(solution)/shard_map/all_gather | solution.py:87
  8.8 251.8 %all-gather.10.cloned.1.call-start = ((), (), s32[]{:S(2)}) async-start(), calls=%async_computation.6 | async-start | bytes 5013504 | tf_op jit(solution)/shard_map/all_gather | solution.py:113
  9.5 322.6 %all-gather.12.cloned.1.call-start = ((), (), s32[]{:S(2)}) async-start(), calls=%async_computation.7 | async-start | bytes 5013504 | tf_op jit(solution)/shard_map/all_gather | solution.py:115
  10.1 702.3 %reduce-scatter.7.cloned.1.call-start = ((), (), s32[]{:S(2)}) async-start(), calls=%async_computation.9 | async-start | bytes 2506752 | tf_op jit(solution)/shard_map/reduce_scatter | solution.py:236
  15.6 76.1 %copy-start.13 = (f32[2080]{0:T(1024)}, f32[2080]{0:T(1024)S(1)}, u32[]{:S(2)}) copy-start(f32[2080]{0:T(1024)S(1)} %div.47) | copy-start | bytes 24964
  260.6 71.5 %copy-start.5 = (bf16[5,416,768]{2,1,0:T(8,128)(2,1)S(1)}, bf16[5,416,768]{2,1,0:T(8,128)(2,1)}, u32[]{:S(2)}) copy-start(bf16[5,416,768]{2,1,0:T(8,128)(2,1)} %param.33) | copy-start | bytes 9584644
  360.5 22.0 %copy-start.20 = (f32[2080]{0:T(1024)S(1)}, f32[2080]{0:T(1024)}, u32[]{:S(2)}) copy-start(f32[2080]{0:T(1024)} %copy-done.19) | copy-start | bytes 24964
  360.5 22.0 %copy-start.1 = (f32[2080,768]{1,0:T(8,128)S(1)}, f32[2080,768]{1,0:T(8,128)}, u32[]{:S(2)}) copy-start(f32[2080,768]{1,0:T(8,128)} %fusion.67) | copy-start | bytes 19169284
  397.5 316.4 %reduce-scatter.9.cloned.1.call-start = ((), (), s32[]{:S(2)}) async-start(), calls=%async_computation.10 | async-start | bytes 10027008 | tf_op jit(solution)/shard_map/reduce_scatter | solution.py:170
  416.6 299.1 %reduce-scatter.11.cloned.1.call-start = ((), (), s32[]{:S(2)}) async-start(), calls=%async_computation.11 | async-start | bytes 10027008 | tf_op jit(solution)/shard_map/reduce_scatter | solution.py:172
  459.5 332.9 %reduce-scatter.5.cloned.1.call-start = ((), (), s32[]{:S(2)}) async-start(), calls=%async_computation.8 | async-start | bytes 7520256 | tf_op jit(solution)/shard_map/reduce_scatter | solution.py:234
  657.7 162.8 %all-reduce.22.cloned.1.call-start = ((), (), s32[]{:S(2)}) async-start(), calls=%async_computation.12 | async-start | bytes 1327104 | tf_op jit(solution)/shard_map/psum | solution.py:246
  662.6 17.1 %copy-start.22 = (f32[2080]{0:T(1024)S(1)}, f32[2080]{0:T(1024)}, u32[]{:S(2)}) copy-start(f32[2080]{0:T(1024)} %copy-done.21) | copy-start | bytes 24964
  684.3 11.6 %slice-start = ((s8[6389760]{0:T(1024)(128)(4,1)}), s8[2195456]{0:T(1024)(128)(4,1)S(1)}, s32[]{:S(2)}) async-start(s8[6389760]{0:T(1024)(128)(4,1)} %bitcast.160), calls=%async_computation.13 | async-start | bytes 4390912
  (30 other events, 200.0 us)
Sparse Core Ops, SparseCore 0:
  10.4 50.2 all-gather.5
  63.0 36.8 all-gather.7
  102.1 51.9 all-gather.9
  156.3 51.6 all-gather.11
  397.6 60.5 reduce-scatter.6
  462.2 110.2 reduce-scatter.8
  576.6 110.8 reduce-scatter.10
  691.5 90.4 reduce-scatter.4
  785.6 34.8 all-reduce.21
